TPU v7x, 32 devices: a whole 2x2x4 slice. The times are simulated.
32 devices in a mesh: grp: 8 (over z, core), blk: 4 (over y, x).
Axes of the slice: x: 2, y: 2, z: 4, core: 2. Of those that a mesh axis runs over, the one named last changes fastest.
Arguments:
- integrals: bfloat16 [8, 128, 128, 128], P(None, 'blk'), may hold values from -0.5 to 0.5
- doubles: bfloat16 [64, 128, 128], P('blk'), may hold values from -0.0059814453 to 0.0059814453
- coulomb: bfloat16 [64, 128, 128], P('blk'), may hold values from -0.1796875 to 0.1796875
- singles: float32 [8, 128], P(None, 'blk'), may hold values from -0.18 to 0.18
- occ_energy: float32 [8], replicated, may hold values from -2 to -0.5
- vir_energy: float32 [128], replicated, may hold values from 0.3 to 3
- triplets: int32 [8, 16, 3], P('grp'), may hold values from 0 to 7
- tile_count: int32 [8], P('grp'), may hold values from 1 to 16, as said below
Outputs:
- triplet_energy: float32 [8, 16], P('grp')
- mean_energy: float32 [], replicated
Inputs may be any that keep to these rules, and one draw needn't show every extreme that they name: `tile_count`: slots with an index below a group's count are live; some group has all 16 slots live.
All inputs are finite; a program needn't handle non-finite values.
Results may differ from a plain program's by a relative error of at most 0.0003.
Values may be sent and summed in bfloat16 or wider, within the bound.
A program may use at most 64 MiB of HBM per device.

v0:
```python
import jax
import jax.numpy as jnp
from jax import lax
from jax.sharding import PartitionSpec as P


def select_blocks(pieces, offset, pair_kj, pair_jk):
    doubles_piece = pieces[0]
    coulomb_piece = pieces[1]
    row_count = doubles_piece.shape[0]
    owned = offset + jnp.arange(row_count, dtype=jnp.int32)
    pick_kj = (pair_kj[:, None] == owned[None, :]).astype(jnp.bfloat16)
    pick_jk = (pair_jk[:, None] == owned[None, :]).astype(jnp.bfloat16)
    flat_doubles = doubles_piece.reshape(row_count, -1)
    flat_coulomb = coulomb_piece.reshape(row_count, -1)
    return (
        jnp.dot(pick_kj, flat_doubles, preferred_element_type=jnp.float32),
        jnp.dot(pick_jk, flat_doubles, preferred_element_type=jnp.float32),
        jnp.dot(pick_jk, flat_coulomb, preferred_element_type=jnp.float32),
    )


def body(integrals, doubles, coulomb, singles, occ_energy, vir_energy, triplets, tile_count):
    occupied = integrals.shape[0]
    width_block = integrals.shape[1]
    width = integrals.shape[3]
    slots = triplets.shape[1]
    second_list = triplets[0, :, 1]
    third_list = triplets[0, :, 2]
    pair_kj = third_list * occupied + second_list
    pair_jk = second_list * occupied + third_list
    own_offset = lax.axis_index("blk") * doubles.shape[0]
    local_blocks = select_blocks((doubles, coulomb), own_offset, pair_kj, pair_jk)
    local_half = (
        local_blocks[0].astype(jnp.bfloat16),
        local_blocks[1].astype(jnp.bfloat16),
        local_blocks[2].astype(jnp.bfloat16),
    )
    picked = (
        lax.psum(local_half[0], "blk").astype(jnp.float32),
        lax.psum(local_half[1], "blk").astype(jnp.float32),
        lax.psum(local_half[2], "blk").astype(jnp.float32),
    )
    doubles_kj = picked[0].astype(jnp.bfloat16).reshape(slots, width, width)
    doubles_jk = picked[1].astype(jnp.bfloat16).reshape(slots, width, width)
    coupling_all = picked[2].reshape(slots, width, width)
    block_offset = lax.axis_index("blk") * width_block
    vir_block = lax.dynamic_slice_in_dim(vir_energy, block_offset, width_block)
    vir_sums = vir_block[:, None, None] + vir_energy[None, :, None] + vir_energy[None, None, :]
    slot_ids = jnp.arange(slots, dtype=jnp.int32)
    contract = (((1,), (1,)), ((), ()))

    def slot_step(slot_index, energies):
        first_occ = triplets[0, slot_index, 0]
        second_occ = triplets[0, slot_index, 1]
        third_occ = triplets[0, slot_index, 2]
        slab = lax.dynamic_index_in_dim(integrals, first_occ, 0, False).reshape(
            width_block * width, width
        )
        block_kj = lax.dynamic_index_in_dim(doubles_kj, slot_index, 0, False)
        block_jk = lax.dynamic_index_in_dim(doubles_jk, slot_index, 0, False)
        coupling = lax.dynamic_index_in_dim(coupling_all, slot_index, 0, False)
        first = lax.dot_general(
            slab, block_kj, contract, preferred_element_type=jnp.float32
        ).reshape(width_block, width, width)
        second = lax.dot_general(
            slab, block_jk, contract, preferred_element_type=jnp.float32
        ).reshape(width_block, width, width)
        connected = first + jnp.transpose(second, (0, 2, 1))
        amp_row = lax.dynamic_index_in_dim(singles, first_occ, 0, False)
        full = connected + amp_row[:, None, None] * coupling[None, :, :]
        occ_sum = occ_energy[first_occ] + occ_energy[second_occ] + occ_energy[third_occ]
        denominator = occ_sum - vir_sums
        value = jnp.sum(full * full / denominator)
        value = jnp.where(slot_index < tile_count[0], value, jnp.float32(0.0))
        return energies + jnp.where(slot_ids == slot_index, value, jnp.float32(0.0))

    energies = lax.fori_loop(0, slots, slot_step, jnp.zeros((slots,), jnp.float32))
    trip_energy = lax.psum(energies, "blk")
    grand_total = lax.psum(jnp.sum(trip_energy), "grp")
    mean_energy = grand_total / (lax.axis_size("grp") * slots)
    return (trip_energy.reshape(1, slots), mean_energy)


def solution(mesh):
    in_specs = (
        P(None, "blk", None, None),
        P("blk", None, None),
        P("blk", None, None),
        P(None, "blk"),
        P(),
        P(),
        P("grp", None, None),
        P("grp"),
    )
    out_specs = (P("grp", None), P())
    return jax.shard_map(body, mesh=mesh, in_specs=in_specs, out_specs=out_specs, check_vma=False)
```

profile of v0, /device:TPU:0, one launch (start us, length us, event | category | flops | bytes accessed | tf_op | source)
XLA Modules:
  0.0 349.9 jit_solution(18228898018324699420)
XLA Ops:
  7.2 0.7 fusion.39
  8.0 1.5 fusion.22
  9.5 0.9 copy.14
  10.8 0.9 copy.16
  12.2 0.9 copy.13
  13.3 63.5 %all-reduce.3.cloned.1.call-done = (bf16[16,128,128]{2,1,0:T(8,128)(2,1)}, bf16[16,128,128]{2,1,0:T(8,128)(2,1)}, bf16[16,128,128]{2,1,0:T(8,128)(2,1)}) async-done(((bf16[16,128,128]{2,1,0:T(8,128)(2,1)}, bf16[16,128,128]{2,1,0:T(8,128)(2,1)}, bf16[16,128,128]{2,1,0:T(8,128)(2,1)}), (bf16[16,128,128]{2,1,0:T(8,128)(2,1)}, bf16[16,128,128]{2,1,0:T(8,128)(2,1)}, ...) | async-done | bytes 1572880 | tf_op jit(solution)/shard_map/psum | solution.py:40
  76.8 1.1 reshape.109
  78.0 238.9 %while.14 = (s32[]{:T(128)}, f32[16]{0:T(128)S(1)}, s32[1]{0:T(128)}, s32[1,16,3]{1,0,2:T(1,128)S(1)}, bf16[8,32,128,128]{3,2,1,0:T(8,128)(2,1)}, /*index=5*/bf1...) while((s32[]{:T(128)}, f32[16]{0:T(128)S(1)}, ...), condition=%wide.region_5.6_spmd.clone, body=%wide.region_3.5_spmd.clone.sunk | while | flops 272629824 | bytes 6572943 | solution.py:78
  86.6 1.7 fusion.54
  88.3 0.7 fusion.56
  89.0 2.7 fusion.57
  99.1 0.6 fusion.55
  101.5 1.7 fusion.54
  103.2 0.7 fusion.56
  103.9 2.7 fusion.57
  114.0 0.6 fusion.55
  116.5 1.7 fusion.54
  118.1 0.7 fusion.56
  118.8 2.7 fusion.57
  131.4 1.7 fusion.54
  133.1 0.7 fusion.56
  133.8 2.7 fusion.57
  146.3 1.7 fusion.54
  148.0 0.7 fusion.56
  148.7 2.7 fusion.57
  161.3 1.7 fusion.54
  162.9 0.7 fusion.56
  163.6 2.7 fusion.57
  173.7 0.6 fusion.55
  176.2 1.7 fusion.54
  177.9 0.7 fusion.56
  178.6 2.7 fusion.57
  188.7 0.6 fusion.55
  191.1 1.7 fusion.54
  192.8 0.7 fusion.56
  193.5 2.7 fusion.57
  203.6 0.6 fusion.55
  206.1 1.7 fusion.54
  207.7 0.7 fusion.56
  208.4 2.7 fusion.57
  218.5 0.6 fusion.55
  221.0 1.7 fusion.54
  222.7 0.7 fusion.56
  223.4 2.7 fusion.57
  235.9 1.7 fusion.54
  237.6 0.7 fusion.56
  238.3 2.7 fusion.57
  250.9 1.7 fusion.54
  252.5 0.7 fusion.56
  253.2 2.7 fusion.57
  265.8 1.7 fusion.54
  267.5 0.7 fusion.56
  268.2 2.7 fusion.57
  280.7 1.7 fusion.54
  282.4 0.7 fusion.56
  283.1 2.7 fusion.57
  295.7 1.7 fusion.54
  297.3 0.7 fusion.56
  298.0 2.7 fusion.57
  310.6 1.7 fusion.54
  312.3 0.7 fusion.56
  313.0 2.7 fusion.57
  316.9 8.9 %psum.38 = f32[16]{0:T(128)S(1)} all-reduce(f32[16]{0:T(128)S(1)} %get-tuple-element.201), channel_id=1, replica_groups=mesh['grp'=8,'blk'=4] {'blk'}, use_global_device_ids=true, to_apply=%region_6.7 | all-reduce | flops 16 | bytes 128 | tf_op jit(solution)/shard_map/psum | solution.py:79
  326.5 14.8 %psum.39 = f32[]{:T(128)} all-reduce(f32[]{:T(128)} %reduce_sum.22), channel_id=1, replica_groups=mesh['grp'=8,'blk'=4] {'grp'}, use_global_device_ids=true, to_apply=%region_8.9 | all-reduce | flops 1 | bytes 8 | tf_op jit(solution)/shard_map/psum | solution.py:80
  (78 shorter events, 18.0 us)
Async XLA Ops:
  7.2 3.2 copy-start.1
  7.2 69.7 %all-reduce.3.cloned.1.call-start = ((), (), s32[]{:S(2)}) async-start(), calls=%async_computation | async-start | bytes 3145728 | tf_op jit(solution)/shard_map/psum | solution.py:40
  8.0 3.8 %copy-start = (bf16[16,128,128]{2,1,0:T(8,128)(2,1)S(1)}, bf16[16,128,128]{2,1,0:T(8,128)(2,1)}, u32[]{:S(2)}) copy-start(bf16[16,128,128]{2,1,0:T(8,128)(2,1)} %param.11) | copy-start | bytes 1572868
  11.7 1.4 copy-start.4
  12.2 65.8 %copy-start.2 = (f32[8]{0:T(128)S(1)}, f32[8]{0:T(128)}, u32[]{:S(2)}) copy-start(f32[8]{0:T(128)} %param.14) | copy-start | bytes 100
  12.2 65.8 %copy-start.3 = (s32[1,16,3]{1,0,2:T(1,128)S(1)}, s32[1,16,3]{1,0,2:T(1,128)}, u32[]{:S(2)}) copy-start(s32[1,16,3]{1,0,2:T(1,128)} %param.16) | copy-start | bytes 580
  325.9 16.0 %copy-start.5 = (f32[16]{0:T(128)}, f32[16]{0:T(128)S(1)}, u32[]{:S(2)}) copy-start(f32[16]{0:T(128)S(1)} %psum.38) | copy-start | bytes 196
Sparse Core Ops, SparseCore 0:
  13.2 63.5 all-reduce.2
where the time goes:
time: 353 us; the launch traced here: 350 us
  loops' own time  138 us (39%)
  matrix products  72.4 us (21%)
  waiting for transfers between devices  63.5 us (18%)
  local copies, waits for them, and re-layouts  33.9 us (10%)
  blocking collectives  23.7 us (7%)
  between operations  15.9 us (5%)
    another operation x1, loops' own time, body(): lax.fori_loop(0, slots, slot_step, jnp.zeros((slots,), jnp.float32))  138 us
    psum x1, waiting for transfers between devices, body(): lax.psum(local_half[0], 'blk').astype(jnp.float32)  63.5 us
    dot_general x16, matrix products, slot_step(): lax.dot_general(slab, block_jk, contract, preferred_element_type=jnp.floa...  43.5 us
    dot_general x16, matrix products, slot_step(): lax.dot_general(slab, block_kj, contract, preferred_element_type=jnp.floa...  26.5 us
    psum x1, blocking collectives, body(): grand_total = lax.psum(jnp.sum(trip_energy), 'grp')  14.8 us
    mul x32, local copies, waits for them, and re-layouts, slot_step(): full = connected + amp_row[:, None, None] * coupling[None, :, :]  11.3 us
    dynamic_slice x16, local copies, waits for them, and re-layouts, slot_step(): occ_energy[third_occ]  9.94 us
    dynamic_slice x16, local copies, waits for them, and re-layouts, slot_step(): third_occ = triplets[0, slot_index, 2]  9.85 us
  transfers between devices with their start and end apart: 1, of which 1 were waited for; matrix products, arithmetic and copies ran while one was open for 0% of the time, Pallas kernels for 0%

commit v1 on v0

--- a/solution.py
+++ b/solution.py
@@ -37,7 +37,7 @@
         local_blocks[2].astype(jnp.bfloat16),
     )
     picked = (
-        lax.psum(local_half[0], "blk").astype(jnp.float32),
+        jnp.sum(lax.all_gather(local_half[0], "blk"), axis=0).astype(jnp.float32),
         lax.psum(local_half[1], "blk").astype(jnp.float32),
         lax.psum(local_half[2], "blk").astype(jnp.float32),
     )

time: 353 us -> 382 us (1.082)
  waiting for transfers between devices: 63.5 us -> 89.8 us
    all_gather x0 -> x1, waiting for transfers between devices: none -> 35.9 us  [body(): lax.all_gather(local_half[0], 'blk')]
    psum x1, waiting for transfers between devices: 63.5 us -> 53.8 us  [body(): lax.psum(local_half[1], 'blk').astype(jnp.float32)]
  transfers between devices with their start and end apart: 1 -> 2, of which waited for: 1 -> 2; matrix products, arithmetic and copies ran while one was open for 0% -> 1% of each run, Pallas kernels for 0% -> 0%
where the time goes in v1:
time: 382 us; the launch traced here: 378 us
  loops' own time  138 us (36%)
  waiting for transfers between devices  89.8 us (24%)
  matrix products  73.1 us (19%)
  local copies, waits for them, and re-layouts  33 us (9%)
  blocking collectives  23.7 us (6%)
  between operations  16 us (4%)
  other arithmetic  4.82 us (1%)
    another operation x1, loops' own time, body(): lax.fori_loop(0, slots, slot_step, jnp.zeros((slots,), jnp.float32))  138 us
    psum x1, waiting for transfers between devices, body(): lax.psum(local_half[1], 'blk').astype(jnp.float32)  53.8 us
    dot_general x16, matrix products, slot_step(): lax.dot_general(slab, block_jk, contract, preferred_element_type=jnp.floa...  43.3 us
    all_gather x1, waiting for transfers between devices, body(): lax.all_gather(local_half[0], 'blk')  35.9 us
    dot_general x16, matrix products, slot_step(): lax.dot_general(slab, block_kj, contract, preferred_element_type=jnp.floa...  26.6 us
    psum x1, blocking collectives, body(): grand_total = lax.psum(jnp.sum(trip_energy), 'grp')  14.8 us
    mul x32, local copies, waits for them, and re-layouts, slot_step(): full = connected + amp_row[:, None, None] * coupling[None, :, :]  11.3 us
    dynamic_slice x16, local copies, waits for them, and re-layouts, slot_step(): occ_energy[third_occ]  9.94 us
  transfers between devices with their start and end apart: 2, of which 2 were waited for; matrix products, arithmetic and copies ran while one was open for 1% of the time, Pallas kernels for 0%

profile of v1, /device:TPU:0, one launch (start us, length us, event | category | flops | bytes accessed | tf_op | source)
XLA Modules:
  0.0 378.1 jit_solution(12367325976329626997)
XLA Ops:
  7.2 0.7 fusion.38
  8.0 1.5 fusion.21
  9.4 0.9 copy.14
  10.8 0.9 copy.16
  11.8 1.2 convolution_convert_fusion.2
  13.2 53.8 %all-reduce.3.cloned.1.call-done = (bf16[16,128,128]{2,1,0:T(8,128)(2,1)}, bf16[16,128,128]{2,1,0:T(8,128)(2,1)}) async-done(((bf16[16,128,128]{2,1,0:T(8,128)(2,1)}, bf16[16,128,128]{2,1,0:T(8,128)(2,1)}), (bf16[16,128,128]{2,1,0:T(8,128)(2,1)}, bf16[16,128,128]{2,1,0:T(8,128)(2,1)})) %all-reduce.3.cloned.1.call-update) | async-done | bytes 1048592 | tf_op jit(solution)/shard_map/psum | solution.py:41
  67.0 1.1 reshape.109
  68.2 35.9 %all-gather.3.cloned.1.call-done = bf16[64,16384]{1,0:T(8,128)(2,1)} async-done(((bf16[16,16384]{1,0:T(8,128)(2,1)}), bf16[64,16384]{1,0:T(8,128)(2,1)}) %all-gather.3.cloned.1.call-update) | async-done | bytes 2097168 | tf_op jit(solution)/shard_map/all_gather | solution.py:40
  104.1 2.1 reduce_sum.34
  106.3 238.9 %while.14 = (s32[]{:T(128)}, f32[16]{0:T(128)S(1)}, s32[1]{0:T(128)}, s32[1,16,3]{1,0,2:T(1,128)S(1)}, bf16[8,32,128,128]{3,2,1,0:T(8,128)(2,1)}, /*index=5*/bf1...) while((s32[]{:T(128)}, f32[16]{0:T(128)S(1)}, ...), condition=%wide.region_5.6_spmd.clone, body=%wide.region_3.5_spmd.clone.sunk | while | flops 272629824 | bytes 6572943 | solution.py:78
  112.4 0.6 fusion.54
  114.9 1.7 fusion.53
  116.6 0.7 fusion.55
  117.3 2.7 fusion.56
  127.4 0.6 fusion.54
  129.8 1.7 fusion.53
  131.5 0.7 fusion.55
  132.2 2.7 fusion.56
  142.3 0.6 fusion.54
  144.8 1.7 fusion.53
  146.4 0.7 fusion.55
  147.1 2.7 fusion.56
  159.7 1.7 fusion.53
  161.4 0.7 fusion.55
  162.1 2.7 fusion.56
  172.2 0.6 fusion.54
  174.6 1.7 fusion.53
  176.3 0.7 fusion.55
  177.0 2.7 fusion.56
  189.6 1.7 fusion.53
  191.2 0.7 fusion.55
  191.9 2.7 fusion.56
  204.5 1.7 fusion.53
  206.2 0.7 fusion.55
  206.9 2.7 fusion.56
  219.4 1.7 fusion.53
  221.1 0.7 fusion.55
  221.8 2.7 fusion.56
  234.3 1.7 fusion.53
  236.0 0.7 fusion.55
  236.7 2.7 fusion.56
  249.3 1.7 fusion.53
  250.9 0.7 fusion.55
  251.6 2.7 fusion.56
  264.2 1.7 fusion.53
  265.9 0.7 fusion.55
  266.6 2.7 fusion.56
  279.1 1.7 fusion.53
  280.8 0.7 fusion.55
  281.5 2.7 fusion.56
  294.1 1.7 fusion.53
  295.7 0.7 fusion.55
  296.4 2.7 fusion.56
  309.0 1.7 fusion.53
  310.7 0.7 fusion.55
  311.4 2.7 fusion.56
  323.9 1.7 fusion.53
  325.6 0.7 fusion.55
  326.3 2.7 fusion.56
  338.9 1.7 fusion.53
  340.5 0.7 fusion.55
  341.2 2.7 fusion.56
  345.2 8.9 %psum.30 = f32[16]{0:T(128)S(1)} all-reduce(f32[16]{0:T(128)S(1)} %get-tuple-element.201), channel_id=1, replica_groups=mesh['grp'=8,'blk'=4] {'blk'}, use_global_device_ids=true, to_apply=%region_6.7 | all-reduce | flops 16 | bytes 128 | tf_op jit(solution)/shard_map/psum | solution.py:79
  354.7 14.8 %psum.31 = f32[]{:T(128)} all-reduce(f32[]{:T(128)} %reduce_sum.35), channel_id=1, replica_groups=mesh['grp'=8,'blk'=4] {'grp'}, use_global_device_ids=true, to_apply=%region_8.9 | all-reduce | flops 1 | bytes 8 | tf_op jit(solution)/shard_map/psum | solution.py:80
  (82 shorter events, 19.0 us)
Async XLA Ops:
  7.2 3.2 copy-start.1
  7.2 59.9 %all-reduce.3.cloned.1.call-start = ((), (), s32[]{:S(2)}) async-start(), calls=%async_computation.1 | async-start | bytes 2097152 | tf_op jit(solution)/shard_map/psum | solution.py:41
  9.4 2.3 copy-start
  10.8 2.3 copy-start.4
  11.7 92.4 %all-gather.3.cloned.1.call-start = ((), (), s32[]{:S(2)}) async-start(), calls=%async_computation | async-start | bytes 2621440 | tf_op jit(solution)/shard_map/all_gather | solution.py:40
  68.2 38.1 %copy-start.2 = (f32[8]{0:T(128)S(1)}, f32[8]{0:T(128)}, u32[]{:S(2)}) copy-start(f32[8]{0:T(128)} %param.14) | copy-start | bytes 100
  68.2 38.1 %copy-start.3 = (s32[1,16,3]{1,0,2:T(1,128)S(1)}, s32[1,16,3]{1,0,2:T(1,128)}, u32[]{:S(2)}) copy-start(s32[1,16,3]{1,0,2:T(1,128)} %param.16) | copy-start | bytes 580
  354.1 16.0 %copy-start.5 = (f32[16]{0:T(128)}, f32[16]{0:T(128)S(1)}, u32[]{:S(2)}) copy-start(f32[16]{0:T(128)S(1)} %psum.30) | copy-start | bytes 196
Sparse Core Ops, SparseCore 0:
  11.8 55.1 all-reduce.2
  68.9 35.1 all-gather.2
